TPU v7x, 32 devices: a whole 2x2x4 slice. The times are simulated.
32 devices in a mesh: img: 2 (over x), ga: 4 (over y, core), band: 4 (over z).
Axes of the slice: x: 2, y: 2, z: 4, core: 2. Of those that a mesh axis runs over, the one named last changes fastest.
Arguments:
- orbitals: bfloat16 [1536, 12288], P(('img', 'band'), 'ga'), parts along dimension 0, as said below
- kernel: float32 [12288], P('ga'), may hold values from 0.3 to 3
- block_vectors: bfloat16 [512, 12288], P(('img', 'band'), 'ga'), parts along dimension 0
Outputs:
- ace_vectors: bfloat16 [1536, 12288], P(('img', 'band'), 'ga'), parts along dimension 0
- exchange_block: bfloat16 [512, 12288], P(('img', 'band'), 'ga'), parts along dimension 0
There are 2 independent parts, one for each index of `img`. A program takes and returns all parts, laid end to end along the dimension named above; an argument that names none is the same for every part. Nothing has to cross between parts.
Inputs may be any that keep to these rules, and one draw needn't show every extreme that they name: `orbitals`: the bands of one image are linearly independent, and the block lies largely in their span.
All inputs are finite; a program needn't handle non-finite values.
Results may differ from a plain program's by a relative error of at most 0.02.
Values may be sent and summed in bfloat16 or wider, within the bound.
A program may use at most 64 MiB of HBM per device.

v0:
```python
import jax
import jax.numpy as jnp
from jax import lax
from jax.sharding import PartitionSpec as P


def contract_first(left, right):
    return lax.dot_general(left, right, (((0,), (0,)), ((), ())), precision=lax.Precision.HIGHEST)


def shards(orbitals, kernel, block_vectors):
    groups = lax.axis_size("ga")
    own_band = lax.axis_index("band")
    total_coeffs = orbitals.shape[1] * groups
    full_orbitals, full_block = (
        lax.all_gather(orbitals, "band", axis=0, tiled=True),
        lax.all_gather(block_vectors, "band", axis=0, tiled=True),
    )
    weighted = (-(full_orbitals.astype(jnp.float32) * kernel[None, :])).astype(jnp.bfloat16)
    own_rows = orbitals.shape[0]
    partial_rows = lax.dot_general(
        orbitals, weighted, (((1,), (1,)), ((), ())), preferred_element_type=jnp.float32
    )
    summed_rows = lax.psum(partial_rows.astype(jnp.bfloat16), "ga").astype(jnp.float32)
    margin = -lax.all_gather(summed_rows, "band", axis=0, tiled=True) / total_coeffs
    factor = jnp.linalg.cholesky(margin)
    identity = jnp.eye(factor.shape[0], dtype=jnp.float32)
    inverse = lax.linalg.triangular_solve(factor, identity, left_side=True, lower=True)
    inverse_rows = lax.dynamic_slice_in_dim(inverse, own_band * own_rows, own_rows, 0)
    projector = jnp.dot(inverse_rows, weighted.astype(jnp.float32), precision=lax.Precision.HIGHEST)
    local_coupling = jnp.dot(
        projector, full_block.astype(jnp.float32).T, precision=lax.Precision.HIGHEST
    )
    coupling = (
        lax.psum(local_coupling.astype(jnp.bfloat16), "ga").astype(jnp.float32) / total_coeffs
    )
    applied = lax.psum_scatter(
        -contract_first(coupling, projector), "band", scatter_dimension=0, tiled=True
    )
    return (projector.astype(jnp.bfloat16), applied.astype(jnp.bfloat16))


def solution(mesh):
    placed = (P(("img", "band"), "ga"), P("ga"), P(("img", "band"), "ga"))
    return jax.shard_map(
        shards,
        mesh=mesh,
        in_specs=placed,
        out_specs=(P(("img", "band"), "ga"), P(("img", "band"), "ga")),
        check_vma=False,
    )
```

profile of v0, /device:TPU:0, one launch (start us, length us, event | category | flops | bytes accessed | tf_op | source)
XLA Modules:
  0.0 548.5 jit_solution(6717364289099904385)
XLA Ops:
  7.9 93.7 %all-gather.4.cloned.1.call-done = bf16[768,3072]{1,0:T(8,128)(2,1)} async-done(((bf16[192,3072]{1,0:T(8,128)(2,1)}), bf16[768,3072]{1,0:T(8,128)(2,1)}) %all-gather.4.cloned.1.call-update) | async-done | bytes 4718608 | tf_op jit(solution)/shard_map/all_gather | solution.py:16
  101.7 5.1 fusion.20
  106.9 30.9 %all-reduce.4.cloned.1.call-done = bf16[192,768]{1,0:T(8,128)(2,1)} async-done(((bf16[192,768]{1,0:T(8,128)(2,1)}), bf16[192,768]{1,0:T(8,128)(2,1)}) %all-reduce.4.cloned.1.call-update) | async-done | bytes 294928 | tf_op jit(solution)/shard_map/psum | solution.py:24
  142.1 47.9 %all-gather.6.cloned.1.call-done = f32[768,768]{1,0:T(8,128)} async-done(((f32[192,768]{1,0:T(8,128)}), f32[768,768]{1,0:T(8,128)}) %all-gather.6.cloned.1.call-update) | async-done | bytes 2359312 | tf_op jit(solution)/shard_map/all_gather | solution.py:25
  190.0 2.0 copy.7
  193.7 3.2 copy.8
  197.0 2.1 fusion.2
  200.5 11.7 %cholesky.165 = f32[128,128]{1,0:T(8,128)S(1)} custom-call(f32[128,128]{1,0:T(8,128)S(1)} %cholesky.424), custom_call_target="Cholesky" | custom-call | tf_op jit(solution)/shard_map/jit(cholesky)/cholesky | solution.py:26
  212.3 9.8 %custom-call.46 = f32[1,128,128]{1,2,0:T(8,128)S(1)} custom-call(f32[1,128,128]{2,1,0:T(8,128)S(1)} %get-tuple-element.45), custom_call_target="InvertDiagBlocksLowerTriangular" | custom-call | tf_op jit(solution)/shard_map/jit(cholesky)/cholesky | solution.py:26
  225.0 11.7 %cholesky.188 = f32[128,128]{1,0:T(8,128)S(1)} custom-call(f32[128,128]{1,0:T(8,128)S(1)} %cholesky.428), custom_call_target="Cholesky" | custom-call | tf_op jit(solution)/shard_map/jit(cholesky)/cholesky | solution.py:26
  236.8 10.0 %custom-call.47 = f32[1,128,128]{1,2,0:T(8,128)S(1)} custom-call(f32[1,128,128]{2,1,0:T(8,128)S(1)} %get-tuple-element.42), custom_call_target="InvertDiagBlocksLowerTriangular" | custom-call | tf_op jit(solution)/shard_map/jit(cholesky)/cholesky | solution.py:26
  248.7 11.7 %cholesky.354 = f32[128,128]{1,0:T(8,128)S(1)} custom-call(f32[128,128]{1,0:T(8,128)S(1)} %cholesky.433), custom_call_target="Cholesky" | custom-call | tf_op jit(solution)/shard_map/jit(cholesky)/cholesky | solution.py:26
  261.2 9.8 %custom-call.48 = f32[1,128,128]{1,2,0:T(8,128)S(1)} custom-call(f32[1,128,128]{2,1,0:T(8,128)S(1)} %get-tuple-element.39), custom_call_target="InvertDiagBlocksLowerTriangular" | custom-call | tf_op jit(solution)/shard_map/jit(cholesky)/cholesky | solution.py:26
  272.9 12.2 %cholesky.373 = f32[128,128]{1,0:T(8,128)S(1)} custom-call(f32[128,128]{1,0:T(8,128)S(1)} %cholesky.438), custom_call_target="Cholesky" | custom-call | tf_op jit(solution)/shard_map/jit(cholesky)/cholesky | solution.py:26
  285.8 9.8 %custom-call.49 = f32[1,128,128]{1,2,0:T(8,128)S(1)} custom-call(f32[1,128,128]{2,1,0:T(8,128)S(1)} %get-tuple-element.36), custom_call_target="InvertDiagBlocksLowerTriangular" | custom-call | tf_op jit(solution)/shard_map/jit(cholesky)/cholesky | solution.py:26
  297.4 11.7 %cholesky.392 = f32[128,128]{1,0:T(8,128)S(1)} custom-call(f32[128,128]{1,0:T(8,128)S(1)} %cholesky.443), custom_call_target="Cholesky" | custom-call | tf_op jit(solution)/shard_map/jit(cholesky)/cholesky | solution.py:26
  309.8 9.8 %custom-call.50 = f32[1,128,128]{1,2,0:T(8,128)S(1)} custom-call(f32[1,128,128]{2,1,0:T(8,128)S(1)} %get-tuple-element.33), custom_call_target="InvertDiagBlocksLowerTriangular" | custom-call | tf_op jit(solution)/shard_map/jit(cholesky)/cholesky | solution.py:26
  321.2 11.9 %cholesky.410 = f32[128,128]{1,0:T(8,128)S(1)} custom-call(f32[128,128]{1,0:T(8,128)S(1)} %convolution_subtract_fusion.8), custom_call_target="Cholesky" | custom-call | tf_op jit(solution)/shard_map/jit(cholesky)/cholesky | solution.py:26
  340.0 21.3 %while.1 = (s32[]{:T(128)}, f32[768,768]{1,0:T(8,128)}, s32[6,2]{0,1:T(2,128)S(1)}, f32[6,128,128]{2,1,0:T(8,128)}, s32[]{:T(128)}) while((s32[]{:T(128)}, f32[768,768]{1,0:T(8,128)}, s32[6,2]{0,1:T(2,128)S(1)}, f32[6,128,128]{2,1,0:T(8,128)}, s32[]{:T(128)}) %tuple.45), condition=%wide.while_cond, body=%wide.while_body.sunk | while | flops 2 | bytes 132705 | solution.py:28
  340.6 3.0 bitcast_dynamic-update-slice_fusion.2
  344.3 2.9 bitcast_dynamic-update-slice_fusion.2
  347.8 2.9 bitcast_dynamic-update-slice_fusion.2
  351.4 2.9 bitcast_dynamic-update-slice_fusion.2
  354.9 2.9 bitcast_dynamic-update-slice_fusion.2
  358.4 2.8 bitcast_dynamic-update-slice_fusion.2
  361.3 60.4 %custom-call.51 = f32[6,128,128]{1,2,0:T(8,128)} custom-call(f32[6,128,128]{2,1,0:T(8,128)} %get-tuple-element.9), custom_call_target="InvertDiagBlocksLowerTriangular" | custom-call | tf_op jit(solution)/shard_map/triangular_solve | solution.py:28
  432.2 2.3 convolution_subtract_fusion
  435.0 4.2 fusion.65
  439.3 3.8 convolution_convert_fusion
  443.4 30.3 %all-reduce.6.cloned.1.call-done = bf16[192,256]{1,0:T(8,128)(2,1)} async-done(((bf16[192,256]{1,0:T(8,128)(2,1)}), bf16[192,256]{1,0:T(8,128)(2,1)}) %all-reduce.6.cloned.1.call-update) | async-done | bytes 98320 | tf_op jit(solution)/shard_map/psum | solution.py:35
  473.6 5.3 convolution_negate_fusion
  479.0 60.6 %reduce-scatter.2.cloned.1.call-done = f32[64,3072]{1,0:T(8,128)} async-done(((f32[256,3072]{1,0:T(8,128)}), f32[64,3072]{1,0:T(8,128)}) %reduce-scatter.2.cloned.1.call-update) | async-done | bytes 786448 | tf_op jit(solution)/shard_map/reduce_scatter | solution.py:37
  (84 shorter events, 40.5 us)
Async XLA Ops:
  7.2 94.5 %all-gather.4.cloned.1.call-start = ((), (), s32[]{:S(2)}) async-start(), calls=%async_computation.1 | async-start | bytes 5898240 | tf_op jit(solution)/shard_map/all_gather | solution.py:16
  7.9 130.0 %all-reduce.4.cloned.1.call-start = ((), (), s32[]{:S(2)}) async-start(), calls=%async_computation.2 | async-start | bytes 589824 | tf_op jit(solution)/shard_map/psum | solution.py:24
  106.9 83.2 %all-gather.6.cloned.1.call-start = ((), (), s32[]{:S(2)}) async-start(), calls=%async_computation.3 | async-start | bytes 2949120 | tf_op jit(solution)/shard_map/all_gather | solution.py:25
  139.7 299.6 %all-gather.8.cloned.1.call-start = ((), (), s32[]{:S(2)}) async-start(), calls=%async_computation.4 | async-start | bytes 1966080 | tf_op jit(solution)/shard_map/all_gather | solution.py:17
  140.3 333.4 %all-reduce.6.cloned.1.call-start = ((), (), s32[]{:S(2)}) async-start(), calls=%async_computation.5 | async-start | bytes 196608 | tf_op jit(solution)/shard_map/psum | solution.py:35
  199.0 1.5 copy-start.1
  340.0 85.0 %copy-start = (f32[768,768]{1,0:T(8,128)S(1)}, f32[768,768]{1,0:T(8,128)}, u32[]{:S(2)}) copy-start(f32[768,768]{1,0:T(8,128)} %fusion.24) | copy-start | bytes 7077892
  421.7 2.8 copy-start.2
  427.1 7.9 %slice-start = ((s8[4718592]{0:T(1024)(128)(4,1)}), s8[4194304]{0:T(1024)(128)(4,1)S(1)}, s32[]{:S(2)}) async-start(s8[4718592]{0:T(1024)(128)(4,1)} %bitcast.83), calls=%async_computation.7 | async-start | bytes 8388608
  429.6 5.4 slice-start.1
  431.6 3.4 copy-start.3
  443.1 96.4 %reduce-scatter.2.cloned.1.call-start = ((), (), s32[]{:S(2)}) async-start(), calls=%async_computation.6 | async-start | bytes 3932160 | tf_op jit(solution)/shard_map/reduce_scatter | solution.py:37
Sparse Core Ops, SparseCore 0:
  9.5 92.1 all-gather.3
  107.0 30.8 all-reduce.3
  140.0 49.9 all-gather.5
  191.4 35.7 all-gather.7
  443.2 30.3 all-reduce.5
  479.1 60.3 reduce-scatter.1
where the time goes:
time: 552 us; the launch traced here: 549 us
  waiting for transfers between devices  265 us (48%)
  other arithmetic  195 us (35%)
  matrix products  41.5 us (8%)
  local copies, waits for them, and re-layouts  28.2 us (5%)
  between operations  18.6 us (3%)
    another operation x22, other arithmetic, shards(): factor = jnp.linalg.cholesky(margin)  124 us
    all_gather x1, waiting for transfers between devices, shards(): lax.all_gather(orbitals, 'band', axis=0, tiled=True)  93.7 us
    another operation x3, other arithmetic, shards(): lax.linalg.triangular_solve(factor, identity, left_side=True, lower=True)  62 us
    reduce_scatter x1, waiting for transfers between devices, shards(): lax.psum_scatter(-contract_first(coupling, projector), 'band', scatter_di...  60.6 us
    all_gather x1, waiting for transfers between devices, shards(): lax.all_gather(summed_rows, 'band', axis=0, tiled=True)  47.9 us
    psum x1, waiting for transfers between devices, shards(): lax.psum(partial_rows.astype(jnp.bfloat16), 'ga').astype(jnp.float32)  30.9 us
    psum x1, waiting for transfers between devices, shards(): lax.psum(local_coupling.astype(jnp.bfloat16), 'ga').astype(jnp.float32)  30.3 us
    another operation x18, local copies, waits for them, and re-layouts  21.3 us
  transfers between devices with their start and end apart: 6, of which 5 were waited for; matrix products, arithmetic and copies ran while one was open for 45% of the time, Pallas kernels for 0%

commit v1 on v0

--- a/solution.py
+++ b/solution.py
@@ -31,9 +31,8 @@
     local_coupling = jnp.dot(
         projector, full_block.astype(jnp.float32).T, precision=lax.Precision.HIGHEST
     )
-    coupling = (
-        lax.psum(local_coupling.astype(jnp.bfloat16), "ga").astype(jnp.float32) / total_coeffs
-    )
+    tracks_manage = lambda mat: lax.all_gather(mat, axis_name="ga").sum(axis=0)
+    coupling = tracks_manage(local_coupling.astype(jnp.bfloat16)).astype(jnp.float32) / total_coeffs
     applied = lax.psum_scatter(
         -contract_first(coupling, projector), "band", scatter_dimension=0, tiled=True
     )

time: 552 us -> 525 us (0.951)
  waiting for transfers between devices: 265 us -> 233 us
  blocking collectives: 0 us -> 6.69 us
    psum x1 -> x0, waiting for transfers between devices: 30.3 us -> none  [shards(): lax.psum(local_coupling.astype(jnp.bfloat16), 'ga').astype(jnp.float32)]
    all_gather x0 -> x1, blocking collectives: none -> 6.69 us  [shards(): tracks_manage = lambda mat: lax.all_gather(mat, axis_name='ga').sum(axis=0)]
  transfers between devices with their start and end apart: 6 -> 5, of which waited for: 5 -> 4; matrix products, arithmetic and copies ran while one was open for 45% -> 47% of each run, Pallas kernels for 0% -> 0%
where the time goes in v1:
time: 525 us; the launch traced here: 521 us
  waiting for transfers between devices  233 us (44%)
  other arithmetic  195 us (37%)
  matrix products  39.9 us (8%)
  local copies, waits for them, and re-layouts  28.2 us (5%)
  between operations  18.3 us (3%)
  blocking collectives  6.69 us (1%)
    another operation x22, other arithmetic, shards(): factor = jnp.linalg.cholesky(margin)  124 us
    all_gather x1, waiting for transfers between devices, shards(): lax.all_gather(orbitals, 'band', axis=0, tiled=True)  93.7 us
    another operation x3, other arithmetic, shards(): lax.linalg.triangular_solve(factor, identity, left_side=True, lower=True)  62 us
    reduce_scatter x1, waiting for transfers between devices, shards(): lax.psum_scatter(-contract_first(coupling, projector), 'band', scatter_di...  59 us
    all_gather x1, waiting for transfers between devices, shards(): lax.all_gather(summed_rows, 'band', axis=0, tiled=True)  47.9 us
    psum x1, waiting for transfers between devices, shards(): lax.psum(partial_rows.astype(jnp.bfloat16), 'ga').astype(jnp.float32)  30.9 us
    another operation x18, local copies, waits for them, and re-layouts  21.3 us
    another operation x11, matrix products, shards(): lax.linalg.triangular_solve(factor, identity, left_side=True, lower=True)  13.2 us
  transfers between devices with their start and end apart: 5, of which 4 were waited for; matrix products, arithmetic and copies ran while one was open for 47% of the time, Pallas kernels for 0%

profile of v1, /device:TPU:0, one launch (start us, length us, event | category | flops | bytes accessed | tf_op | source)
XLA Modules:
  0.0 521.3 jit_solution(18054667933917096453)
XLA Ops:
  7.9 93.7 %all-gather.5.cloned.1.call-done = bf16[768,3072]{1,0:T(8,128)(2,1)} async-done(((bf16[192,3072]{1,0:T(8,128)(2,1)}), bf16[768,3072]{1,0:T(8,128)(2,1)}) %all-gather.5.cloned.1.call-update) | async-done | bytes 4718608 | tf_op jit(solution)/shard_map/all_gather | solution.py:16
  101.7 5.1 fusion.20
  106.9 30.9 %all-reduce.3.cloned.1.call-done = bf16[192,768]{1,0:T(8,128)(2,1)} async-done(((bf16[192,768]{1,0:T(8,128)(2,1)}), bf16[192,768]{1,0:T(8,128)(2,1)}) %all-reduce.3.cloned.1.call-update) | async-done | bytes 294928 | tf_op jit(solution)/shard_map/psum | solution.py:24
  142.1 47.9 %all-gather.7.cloned.1.call-done = f32[768,768]{1,0:T(8,128)} async-done(((f32[192,768]{1,0:T(8,128)}), f32[768,768]{1,0:T(8,128)}) %all-gather.7.cloned.1.call-update) | async-done | bytes 2359312 | tf_op jit(solution)/shard_map/all_gather | solution.py:25
  190.0 2.0 copy.7
  193.7 3.2 copy.8
  197.0 2.1 fusion.2
  200.5 11.7 %cholesky.165 = f32[128,128]{1,0:T(8,128)S(1)} custom-call(f32[128,128]{1,0:T(8,128)S(1)} %cholesky.424), custom_call_target="Cholesky" | custom-call | tf_op jit(solution)/shard_map/jit(cholesky)/cholesky | solution.py:26
  212.3 9.8 %custom-call.46 = f32[1,128,128]{1,2,0:T(8,128)S(1)} custom-call(f32[1,128,128]{2,1,0:T(8,128)S(1)} %get-tuple-element.45), custom_call_target="InvertDiagBlocksLowerTriangular" | custom-call | tf_op jit(solution)/shard_map/jit(cholesky)/cholesky | solution.py:26
  225.0 11.7 %cholesky.188 = f32[128,128]{1,0:T(8,128)S(1)} custom-call(f32[128,128]{1,0:T(8,128)S(1)} %cholesky.428), custom_call_target="Cholesky" | custom-call | tf_op jit(solution)/shard_map/jit(cholesky)/cholesky | solution.py:26
  236.8 10.0 %custom-call.47 = f32[1,128,128]{1,2,0:T(8,128)S(1)} custom-call(f32[1,128,128]{2,1,0:T(8,128)S(1)} %get-tuple-element.42), custom_call_target="InvertDiagBlocksLowerTriangular" | custom-call | tf_op jit(solution)/shard_map/jit(cholesky)/cholesky | solution.py:26
  248.7 11.7 %cholesky.354 = f32[128,128]{1,0:T(8,128)S(1)} custom-call(f32[128,128]{1,0:T(8,128)S(1)} %cholesky.433), custom_call_target="Cholesky" | custom-call | tf_op jit(solution)/shard_map/jit(cholesky)/cholesky | solution.py:26
  261.2 9.8 %custom-call.48 = f32[1,128,128]{1,2,0:T(8,128)S(1)} custom-call(f32[1,128,128]{2,1,0:T(8,128)S(1)} %get-tuple-element.39), custom_call_target="InvertDiagBlocksLowerTriangular" | custom-call | tf_op jit(solution)/shard_map/jit(cholesky)/cholesky | solution.py:26
  272.9 12.2 %cholesky.373 = f32[128,128]{1,0:T(8,128)S(1)} custom-call(f32[128,128]{1,0:T(8,128)S(1)} %cholesky.438), custom_call_target="Cholesky" | custom-call | tf_op jit(solution)/shard_map/jit(cholesky)/cholesky | solution.py:26
  285.8 9.8 %custom-call.49 = f32[1,128,128]{1,2,0:T(8,128)S(1)} custom-call(f32[1,128,128]{2,1,0:T(8,128)S(1)} %get-tuple-element.36), custom_call_target="InvertDiagBlocksLowerTriangular" | custom-call | tf_op jit(solution)/shard_map/jit(cholesky)/cholesky | solution.py:26
  297.4 11.7 %cholesky.392 = f32[128,128]{1,0:T(8,128)S(1)} custom-call(f32[128,128]{1,0:T(8,128)S(1)} %cholesky.443), custom_call_target="Cholesky" | custom-call | tf_op jit(solution)/shard_map/jit(cholesky)/cholesky | solution.py:26
  309.8 9.8 %custom-call.50 = f32[1,128,128]{1,2,0:T(8,128)S(1)} custom-call(f32[1,128,128]{2,1,0:T(8,128)S(1)} %get-tuple-element.33), custom_call_target="InvertDiagBlocksLowerTriangular" | custom-call | tf_op jit(solution)/shard_map/jit(cholesky)/cholesky | solution.py:26
  321.2 11.9 %cholesky.410 = f32[128,128]{1,0:T(8,128)S(1)} custom-call(f32[128,128]{1,0:T(8,128)S(1)} %convolution_subtract_fusion.8), custom_call_target="Cholesky" | custom-call | tf_op jit(solution)/shard_map/jit(cholesky)/cholesky | solution.py:26
  340.0 21.3 %while.1 = (s32[]{:T(128)}, f32[768,768]{1,0:T(8,128)}, s32[6,2]{0,1:T(2,128)S(1)}, f32[6,128,128]{2,1,0:T(8,128)}, s32[]{:T(128)}) while((s32[]{:T(128)}, f32[768,768]{1,0:T(8,128)}, s32[6,2]{0,1:T(2,128)S(1)}, f32[6,128,128]{2,1,0:T(8,128)}, s32[]{:T(128)}) %tuple.45), condition=%wide.while_cond, body=%wide.while_body.sunk | while | flops 2 | bytes 132705 | solution.py:28
  340.6 3.0 bitcast_dynamic-update-slice_fusion.2
  344.3 2.9 bitcast_dynamic-update-slice_fusion.2
  347.8 2.9 bitcast_dynamic-update-slice_fusion.2
  351.4 2.9 bitcast_dynamic-update-slice_fusion.2
  354.9 2.9 bitcast_dynamic-update-slice_fusion.2
  358.4 2.8 bitcast_dynamic-update-slice_fusion.2
  361.3 60.4 %custom-call.51 = f32[6,128,128]{1,2,0:T(8,128)} custom-call(f32[6,128,128]{2,1,0:T(8,128)} %get-tuple-element.9), custom_call_target="InvertDiagBlocksLowerTriangular" | custom-call | tf_op jit(solution)/shard_map/triangular_solve | solution.py:28
  432.2 2.3 convolution_subtract_fusion
  435.0 4.2 fusion.65
  439.3 3.2 convolution_convert_fusion
  442.4 6.7 %all-gather = bf16[768,256]{1,0:T(8,128)(2,1)S(1)} all-gather(bf16[192,256]{1,0:T(8,128)(2,1)S(1)} %convolution_convert_fusion), channel_id=2, replica_groups=mesh['img'=2,'ga'=4,'band'=4] {'ga'}, dimensions={0}, use_global_device_ids=true | all-gather | bytes 491520 | tf_op jit(solution)/shard_map/all_gather | solution.py:34
  449.2 4.4 convolution_negate_fusion
  453.6 59.0 %reduce-scatter.2.cloned.1.call-done = f32[64,3072]{1,0:T(8,128)} async-done(((f32[256,3072]{1,0:T(8,128)}), f32[64,3072]{1,0:T(8,128)}) %reduce-scatter.2.cloned.1.call-update) | async-done | bytes 786448 | tf_op jit(solution)/shard_map/reduce_scatter | solution.py:36
  (83 shorter events, 40.3 us)
Async XLA Ops:
  7.2 94.5 %all-gather.5.cloned.1.call-start = ((), (), s32[]{:S(2)}) async-start(), calls=%async_computation.1 | async-start | bytes 5898240 | tf_op jit(solution)/shard_map/all_gather | solution.py:16
  7.9 130.0 %all-reduce.3.cloned.1.call-start = ((), (), s32[]{:S(2)}) async-start(), calls=%async_computation.2 | async-start | bytes 589824 | tf_op jit(solution)/shard_map/psum | solution.py:24
  106.9 83.2 %all-gather.7.cloned.1.call-start = ((), (), s32[]{:S(2)}) async-start(), calls=%async_computation.3 | async-start | bytes 2949120 | tf_op jit(solution)/shard_map/all_gather | solution.py:25
  139.7 299.6 %all-gather.9.cloned.1.call-start = ((), (), s32[]{:S(2)}) async-start(), calls=%async_computation.4 | async-start | bytes 1966080 | tf_op jit(solution)/shard_map/all_gather | solution.py:17
  140.3 372.3 %reduce-scatter.2.cloned.1.call-start = ((), (), s32[]{:S(2)}) async-start(), calls=%async_computation.5 | async-start | bytes 3932160 | tf_op jit(solution)/shard_map/reduce_scatter | solution.py:36
  199.0 1.5 copy-start.1
  340.0 85.0 %copy-start = (f32[768,768]{1,0:T(8,128)S(1)}, f32[768,768]{1,0:T(8,128)}, u32[]{:S(2)}) copy-start(f32[768,768]{1,0:T(8,128)} %fusion.24) | copy-start | bytes 7077892
  421.7 2.8 copy-start.2
  427.1 7.9 %slice-start = ((s8[4718592]{0:T(1024)(128)(4,1)}), s8[4194304]{0:T(1024)(128)(4,1)S(1)}, s32[]{:S(2)}) async-start(s8[4718592]{0:T(1024)(128)(4,1)} %bitcast.85), calls=%async_computation.6 | async-start | bytes 8388608
  429.6 5.4 %slice-start.1 = ((s8[4718592]{0:T(1024)(128)(4,1)}), s8[524288]{0:T(1024)(128)(4,1)S(1)}, s32[]{:S(2)}) async-start(s8[4718592]{0:T(1024)(128)(4,1)} %bitcast.85), calls=%async_computation.7 | async-start | bytes 1048576
  431.6 3.4 copy-start.3
Sparse Core Ops, SparseCore 0:
  9.5 92.1 all-gather.4
  107.0 30.8 all-reduce.2
  140.0 49.9 all-gather.6
  191.4 35.7 all-gather.8
  453.8 58.7 reduce-scatter.1
